TPU v7x, 32 devices: a whole 2x2x4 slice. The times are simulated.
32 devices in a mesh: tm: 8 (over z, x), space: 4 (over y, core).
Axes of the slice: x: 2, y: 2, z: 4, core: 2. Of those that a mesh axis runs over, the one named last changes fastest.
Arguments:
- state: float32 [32, 16, 64, 128], P('tm', 'space'), may hold values from -6 to 6
- source: float32 [32, 16, 64, 128], P('tm', 'space'), may hold values from -6 to 6
- absorption: float32 [16, 64, 128], P('space'), may hold values from 0.05 to 0.5
Outputs:
- relaxed: float32 [32, 16, 64, 128], P('tm', 'space')
- coarse_residual: float32 [8, 16, 64, 128], P('tm', 'space')
- residual_norm: float32 [], replicated
All inputs are finite; a program needn't handle non-finite values.
Results may differ from a plain program's by a relative error of at most 0.0004.
Values sent between devices are 32-bit elements; how exact they have to be, the bound alone decides.
A program may use at most 64 MiB of HBM per device.

v0:
```python
import math
import jax
import jax.numpy as jnp
from jax import lax
from jax.sharding import PartitionSpec as P

CF = 4
SWEEPS = 5
coupling = 4.0


def shifted(value, axis, by):
    count = lax.axis_size(axis)
    pairs = [(i, i + by) for i in range(count) if 0 <= i + by < count]
    return lax.ppermute(value, axis, pairs)


def sweep_weights(count):
    spread = 6.0 * coupling / (1.0 + 6.0 * coupling)
    return [
        1.0 / (1.0 + spread * math.cos(math.pi * (2 * k + 1) / (2 * count))) for k in range(count)
    ]


def apply_inner(extended, diag):
    inner = extended[1:-1]
    sides = jnp.pad(inner, ((0, 0), (1, 1), (1, 1)))
    beside = extended[2:] + extended[:-2]
    beside = beside + sides[:, 2:, 1:-1] + sides[:, :-2, 1:-1]
    beside = beside + sides[:, 1:-1, 2:] + sides[:, 1:-1, :-2]
    return diag * inner - coupling * beside


def step_whole(rhs, diag_full):
    field = rhs / diag_full
    for weight in sweep_weights(SWEEPS):
        extended = jnp.pad(field, ((1, 1), (0, 0), (0, 0)))
        field = field + weight * (rhs - apply_inner(extended, diag_full)) / diag_full
    return field


def local(state, source, absorption):
    depth_cells = absorption.shape[0]
    offset = lax.axis_index("space") * depth_cells

    def previous(last):
        return shifted(last, "tm", 1)

    stacked = jnp.concatenate([state[:1], source, absorption[None]], axis=0)
    gathered = lax.all_gather(stacked, "space", axis=1, tiled=True)
    source_full = gathered[1 : CF + 1]
    diag_full = 1.0 + 6.0 * coupling + gathered[CF + 1]

    def own_layers(field):
        return lax.dynamic_slice_in_dim(field, offset, depth_cells, 0)

    def back_full(last):
        return lax.all_gather(previous(own_layers(last)), "space", axis=0, tiled=True)

    points = [gathered[0]] + [None] * (CF - 1)

    def relax_full(points):
        for j in range(1, CF):
            points[j] = step_whole(points[j - 1], diag_full) + source_full[j]
        return points

    points = relax_full(points)
    points[0] = step_whole(back_full(points[-1]), diag_full) + source_full[0]
    points = relax_full(points)
    coarse_full = source_full[0] + step_whole(back_full(points[-1]), diag_full) - points[0]
    coarse_residual = own_layers(coarse_full)
    points = [own_layers(point) for point in points]
    residual_norm = lax.psum(jnp.sum(coarse_residual * coarse_residual), ("tm", "space"))
    relaxed = jnp.stack(points, axis=0)
    return (relaxed, coarse_residual[None], residual_norm)


def solution(mesh):
    return jax.shard_map(
        local,
        mesh=mesh,
        in_specs=(
            P("tm", "space", None, None),
            P("tm", "space", None, None),
            P("space", None, None),
        ),
        out_specs=(P("tm", "space", None, None), P("tm", "space", None, None), P()),
        check_vma=False,
    )
```

profile of v0, /device:TPU:0, one launch (start us, length us, event | category | flops | bytes accessed | tf_op | source)
XLA Modules:
  0.0 141.3 jit_solution(12284245266139244024)
XLA Ops:
  7.2 0.0 all-gather.2.cloned.1.call-start
  7.2 0.9 slice.790
  8.1 2.1 %pad_maximum_fusion = f32[6,4,64,128]{3,2,1,0:T(8,128)} fusion(f32[1,4,64,128]{3,2,1,0:T(8,128)} %bitcast.153, f32[4,4,64,128]{3,2,1,0:T(8,128)} %param.4, f32[1,4,64,128]{3,2,1,0:T(8,128)S(1)} %slice.790), kind=kLoop, calls=%fused_computation.160 | loop fusion | flops 393216 | bytes 1572864 | tf_op jit(solution)/shard_map/concatenate | solution.py:49
  10.2 0.0 all-gather.2.cloned.1.call-update
  10.2 31.4 %all-gather.2.cloned.1.call-done = f32[6,16,64,128]{3,2,1,0:T(8,128)} async-done(((f32[6,4,64,128]{3,2,1,0:T(8,128)}), f32[6,16,64,128]{3,2,1,0:T(8,128)}) %all-gather.2.cloned.1.call-update) | async-done | bytes 3145744 | tf_op jit(solution)/shard_map/all_gather | solution.py:50
  41.6 0.0 copy-start
  41.6 1.4 %fusion.424 = f32[16,64,128]{2,1,0:T(8,128)S(1)} fusion(f32[6,16,64,128]{3,2,1,0:T(8,128)} %all-gather.2.cloned.1.call-done), kind=kLoop, calls=%fused_computation.672 | loop fusion | flops 262144 | bytes 1572864 | tf_op jit(solution)/shard_map/div | solution.py:35
  43.1 1.6 %fusion.10 = f32[16,64,128]{2,1,0:T(8,128)S(1)} fusion(f32[16,64,128]{2,1,0:T(8,128)S(1)} %fusion.424, f32[6,16,64,128]{3,2,1,0:T(8,128)} %all-gather.2.cloned.1.call-done), kind=kLoop, calls=%fused_computation.251 | loop fusion | flops 1703936 | bytes 2097152 | tf_op jit(solution)/shard_map/add | solution.py:38
  44.7 0.0 copy-done
  44.7 0.4 fusion.21
  45.2 0.4 fusion.31
  45.6 0.4 fusion.42
  46.0 0.4 fusion.443
  46.5 0.4 fusion.65
  46.9 0.4 fusion.76
  47.3 0.4 fusion.86
  47.8 0.4 fusion.97
  48.2 0.4 fusion.441
  48.7 0.4 fusion.120
  49.1 0.4 fusion.131
  49.5 0.4 fusion.141
  50.0 0.5 fusion.439
  50.5 0.3 fusion.158
  50.8 0.2 slice_bitcast_fusion
  51.0 0.1 fusion.432
  51.1 3.4 %collective-permute-start = (f32[4,64,128]{2,1,0:T(8,128)S(1)}, f32[4,64,128]{2,1,0:T(8,128)S(1)}, u32[]{:S(2)}, u32[]{:S(2)}) collective-permute-start(f32[4,64,128]{2,1,0:T(8,128)S(1)} %fusion.432), channel_id=1, source_target_pairs={{0,4},{4,8},{8,12},{12,16},{16,20},{20,24},{24,28},{1,5},{5,9},{9,... | collective-permute-start | bytes 393224 | tf_op jit(solution)/shard_map/ppermute | solution.py:15
  54.5 3.1 %collective-permute-done = f32[4,64,128]{2,1,0:T(8,128)S(1)} collective-permute-done((f32[4,64,128]{2,1,0:T(8,128)S(1)}, f32[4,64,128]{2,1,0:T(8,128)S(1)}, u32[]{:S(2)}, u32[]{:S(2)}) %collective-permute-start) | collective-permute-done | bytes 131104 | tf_op jit(solution)/shard_map/ppermute | solution.py:15
  57.6 6.7 %all_gather.10 = f32[16,64,128]{2,1,0:T(8,128)S(1)} all-gather(f32[4,64,128]{2,1,0:T(8,128)S(1)} %collective-permute-done), channel_id=1, replica_groups=mesh['tm'=8,'space'=4] {'space'}, dimensions={0}, use_global_device_ids=true | all-gather | bytes 655360 | tf_op jit(solution)/shard_map/all_gather | solution.py:58
  64.3 0.1 fusion.438
  64.4 0.4 fusion.169
  64.8 0.4 fusion.180
  65.2 0.4 fusion.190
  65.7 0.4 fusion.201
  66.1 0.4 fusion.435
  66.6 0.4 fusion.224
  67.0 0.4 fusion.235
  67.4 0.4 fusion.245
  67.9 0.4 fusion.256
  68.3 0.4 fusion.442
  68.8 0.4 fusion.279
  69.2 0.4 fusion.290
  69.6 0.4 fusion.300
  70.1 0.4 fusion.311
  70.5 0.4 fusion.436
  71.0 0.4 fusion.334
  71.4 0.4 fusion.345
  71.8 0.4 fusion.355
  72.3 0.5 fusion.440
  72.8 0.3 fusion.372
  73.1 0.1 dynamic-slice_bitcast_fusion.1
  73.2 4.4 %collective-permute-start.1 = (f32[4,64,128]{2,1,0:T(8,128)S(1)}, f32[4,64,128]{2,1,0:T(8,128)S(1)}, u32[]{:S(2)}, u32[]{:S(2)}) collective-permute-start(f32[4,64,128]{2,1,0:T(8,128)S(1)} %get-tuple-element.24), channel_id=1, source_target_pairs={{0,4},{4,8},{8,12},{12,16},{16,20},{20,24},{24,28},{1,5},{5,9},{9,... | collective-permute-start | bytes 393224 | tf_op jit(solution)/shard_map/ppermute | solution.py:15
  77.6 3.2 %collective-permute-done.1 = f32[4,64,128]{2,1,0:T(8,128)S(1)} collective-permute-done((f32[4,64,128]{2,1,0:T(8,128)S(1)}, f32[4,64,128]{2,1,0:T(8,128)S(1)}, u32[]{:S(2)}, u32[]{:S(2)}) %collective-permute-start.1) | collective-permute-done | bytes 131104 | tf_op jit(solution)/shard_map/ppermute | solution.py:15
  80.8 6.9 %all_gather.11 = f32[16,64,128]{2,1,0:T(8,128)S(1)} all-gather(f32[4,64,128]{2,1,0:T(8,128)S(1)} %collective-permute-done.1), channel_id=1, replica_groups=mesh['tm'=8,'space'=4] {'space'}, dimensions={0}, use_global_device_ids=true | all-gather | bytes 655360 | tf_op jit(solution)/shard_map/all_gather | solution.py:58
  87.7 0.1 fusion.437
  87.8 0.4 fusion.383
  88.3 0.4 fusion.394
  88.7 0.5 fusion.404
  89.2 0.4 fusion.415
  89.6 0.4 fusion.422
  90.0 1.3 multiply_reduce_fusion
  91.3 42.3 %psum.7 = f32[]{:T(128)} all-reduce(f32[]{:T(128)} %get-tuple-element.3), channel_id=1, replica_groups=mesh['tm'=8,'space'=4] {'tm','space'}, use_global_device_ids=true, to_apply=%region_1.2 | all-reduce | flops 1 | bytes 8 | tf_op jit(solution)/shard_map/psum | solution.py:73
  133.6 0.8 pad_maximum_fusion.1
  (1 shorter events, 0.0 us)
Async XLA Ops:
  7.2 34.5 %all-gather.2.cloned.1.call-start = ((), (), s32[]{:S(2)}) async-start(), calls=%async_computation | async-start | bytes 3932160 | tf_op jit(solution)/shard_map/all_gather | solution.py:50
  41.6 3.1 %copy-start = (f32[6,16,64,128]{3,2,1,0:T(8,128)S(1)}, f32[6,16,64,128]{3,2,1,0:T(8,128)}, u32[]{:S(2)}) copy-start(f32[6,16,64,128]{3,2,1,0:T(8,128)} %all-gather.2.cloned.1.call-done) | copy-start | bytes 9437188
  51.1 6.5 %collective-permute-start = (f32[4,64,128]{2,1,0:T(8,128)S(1)}, f32[4,64,128]{2,1,0:T(8,128)S(1)}, u32[]{:S(2)}, u32[]{:S(2)}) collective-permute-start(f32[4,64,128]{2,1,0:T(8,128)S(1)} %fusion.432), channel_id=1, source_target_pairs={{0,4},{4,8},{8,12},{12,16},{16,20},{20,24},{24,28},{1,5},{5,9},{9,... | collective-permute-start | bytes 393224 | tf_op jit(solution)/shard_map/ppermute | solution.py:15
  73.2 7.6 %collective-permute-start.1 = (f32[4,64,128]{2,1,0:T(8,128)S(1)}, f32[4,64,128]{2,1,0:T(8,128)S(1)}, u32[]{:S(2)}, u32[]{:S(2)}) collective-permute-start(f32[4,64,128]{2,1,0:T(8,128)S(1)} %get-tuple-element.24), channel_id=1, source_target_pairs={{0,4},{4,8},{8,12},{12,16},{16,20},{20,24},{24,28},{1,5},{5,9},{9,... | collective-permute-start | bytes 393224 | tf_op jit(solution)/shard_map/ppermute | solution.py:15
Sparse Core Ops, SparseCore 0:
  10.4 31.2 all-gather.1
where the time goes:
time: 142 us; the launch traced here: 141 us
  blocking collectives  55.8 us (39%)
  waiting for transfers between devices  37.7 us (27%)
  other arithmetic  24.6 us (17%)
  between operations  14.3 us (10%)
  starting transfers between devices  7.81 us (6%)
    psum x1, blocking collectives, local(): lax.psum(jnp.sum(coarse_residual * coarse_residual), ('tm', 'space'))  42.3 us
    all_gather x1, waiting for transfers between devices, local(): gathered = lax.all_gather(stacked, 'space', axis=1, tiled=True)  31.4 us
    add x30, other arithmetic, step_whole(): field + weight * (rhs - apply_inner(extended, diag_full)) / diag_full  14.2 us
    all_gather x2, blocking collectives, back_full(): lax.all_gather(previous(own_layers(last)), 'space', axis=0, tiled=True)  13.5 us
    ppermute x2, starting transfers between devices, shifted(): return lax.ppermute(value, axis, pairs)  7.77 us
    ppermute x2, waiting for transfers between devices, shifted(): return lax.ppermute(value, axis, pairs)  6.35 us
    div x8, other arithmetic, step_whole(): field = rhs / diag_full  3.89 us
  transfers between devices with their start and end apart: 3, of which 3 were waited for; matrix products, arithmetic and copies ran while one was open for 0% of the time, Pallas kernels for 0%

commit v1 on v0

--- a/solution.py
+++ b/solution.py
@@ -1,3 +1,4 @@
+import functools
 import math
 import jax
 import jax.numpy as jnp
@@ -7,6 +8,21 @@
 CF = 4
 SWEEPS = 5
 coupling = 4.0
+
+
+def node_write(mine_x, dim_no):
+    extent = lax.axis_size("space")
+    tray = list(map(lambda pp: (pp, (pp + 1) % extent), range(extent)))
+    x_new = [None] * extent
+    x_new[extent - 1] = mine_x
+    for jj in range(extent - 2, -1, -1):
+        x_new[jj] = lax.ppermute(x_new[jj + 1], "space", tray)
+    field_out = jnp.concatenate(x_new, axis=dim_no)
+    later = (lax.axis_index("space") + 1) * mine_x.shape[dim_no]
+    return jnp.roll(field_out, later, axis=dim_no)
+
+
+seats_all_close = functools.partial(node_write, dim_no=1)
 
 
 def shifted(value, axis, by):
@@ -47,7 +63,7 @@
         return shifted(last, "tm", 1)
 
     stacked = jnp.concatenate([state[:1], source, absorption[None]], axis=0)
-    gathered = lax.all_gather(stacked, "space", axis=1, tiled=True)
+    gathered = seats_all_close(stacked)
     source_full = gathered[1 : CF + 1]
     diag_full = 1.0 + 6.0 * coupling + gathered[CF + 1]
 

time: 142 us -> 134 us (0.944)
  between operations: 14.3 us -> 1.1 us
  waiting for transfers between devices: 37.7 us -> 40.2 us
    ppermute x0 -> x3, waiting for transfers between devices: none -> 34.4 us  [node_write(): x_new[jj] = lax.ppermute(x_new[jj + 1], 'space', tray)]
    all_gather x1 -> x0, waiting for transfers between devices: 31.4 us -> none  [local(): gathered = lax.all_gather(stacked, 'space', axis=1, tiled=True)]
    div x8, other arithmetic: 3.89 us -> 5.79 us  [step_whole(): field = rhs / diag_full]
  transfers between devices with their start and end apart: 3 -> 5, of which waited for: 3 -> 5; matrix products, arithmetic and copies ran while one was open for 0% -> 0% of each run, Pallas kernels for 0% -> 0%
where the time goes in v1:
time: 134 us
  blocking collectives  56.3 us (42%)
  waiting for transfers between devices  40.2 us (30%)
  other arithmetic  24.6 us (18%)
  starting transfers between devices  9.09 us (7%)
  local copies, waits for them, and re-layouts  2.32 us (2%)
    psum x1, blocking collectives, local(): lax.psum(jnp.sum(coarse_residual * coarse_residual), ('tm', 'space'))  42.5 us
    ppermute x3, waiting for transfers between devices, node_write(): x_new[jj] = lax.ppermute(x_new[jj + 1], 'space', tray)  34.4 us
    all_gather x2, blocking collectives, back_full(): lax.all_gather(previous(own_layers(last)), 'space', axis=0, tiled=True)  13.9 us
    add x30, other arithmetic, step_whole(): field + weight * (rhs - apply_inner(extended, diag_full)) / diag_full  13.3 us
    ppermute x2, starting transfers between devices, shifted(): return lax.ppermute(value, axis, pairs)  8.54 us
    div x8, other arithmetic, step_whole(): field = rhs / diag_full  5.79 us
    ppermute x2, waiting for transfers between devices, shifted(): return lax.ppermute(value, axis, pairs)  5.71 us
  transfers between devices with their start and end apart: 5, of which 5 were waited for; matrix products, arithmetic and copies ran while one was open for 0% of the time, Pallas kernels for 0%

profile of v1, /device:TPU:0, one launch (start us, length us, event | category | flops | bytes accessed | tf_op | source)
XLA Modules:
  0.0 133.6 jit_solution(3934758007386616674)
XLA Ops:
  0.6 0.9 slice.790
  1.5 1.2 pad_maximum_fusion
  2.7 0.5 collective-permute-start
  3.3 11.6 %collective-permute-done = f32[6,4,64,128]{3,2,1,0:T(8,128)S(1)} collective-permute-done((f32[6,4,64,128]{3,2,1,0:T(8,128)S(1)}, f32[6,4,64,128]{3,2,1,0:T(8,128)S(1)}, u32[]{:S(2)}, u32[]{:S(2)}) %collective-permute-start) | collective-permute-done | bytes 786464 | tf_op jit(solution)/shard_map/ppermute | solution.py:19
  14.9 11.4 %collective-permute-done.1 = f32[6,4,64,128]{3,2,1,0:T(8,128)S(1)} collective-permute-done((f32[6,4,64,128]{3,2,1,0:T(8,128)S(1)}, f32[6,4,64,128]{3,2,1,0:T(8,128)S(1)}, u32[]{:S(2)}, u32[]{:S(2)}) %collective-permute-start.1) | collective-permute-done | bytes 786464 | tf_op jit(solution)/shard_map/ppermute | solution.py:19
  26.3 11.4 %collective-permute-done.2 = f32[6,4,64,128]{3,2,1,0:T(8,128)S(1)} collective-permute-done((f32[6,4,64,128]{3,2,1,0:T(8,128)S(1)}, f32[6,4,64,128]{3,2,1,0:T(8,128)S(1)}, u32[]{:S(2)}, u32[]{:S(2)}) %collective-permute-start.2) | collective-permute-done | bytes 786464 | tf_op jit(solution)/shard_map/ppermute | solution.py:19
  37.8 0.1 constant_dynamic-update-slice_fusion.6
  37.9 0.1 constant_dynamic-update-slice_fusion.5
  38.0 0.8 copy-done.1
  38.9 0.1 constant_dynamic-update-slice_fusion.3
  39.0 0.1 constant_dynamic-update-slice_fusion.2
  39.1 0.1 constant_dynamic-update-slice_fusion.1
  39.3 0.1 fusion.424
  39.4 0.5 fusion.10
  39.9 0.5 fusion.21
  40.3 0.5 fusion.31
  40.8 0.5 fusion.42
  41.2 0.5 fusion.448
  41.7 0.4 fusion.65
  42.1 0.4 fusion.76
  42.6 0.5 fusion.86
  43.0 0.4 fusion.97
  43.5 0.5 fusion.446
  44.0 0.4 fusion.120
  44.4 0.4 fusion.131
  44.8 0.5 fusion.141
  45.3 0.5 fusion.444
  45.8 0.3 fusion.158
  46.2 4.2 %collective-permute-start.3 = (f32[4,64,128]{2,1,0:T(8,128)S(1)}, f32[4,64,128]{2,1,0:T(8,128)S(1)}, u32[]{:S(2)}, u32[]{:S(2)}) collective-permute-start(f32[4,64,128]{2,1,0:T(8,128)S(1)} %fusion.432), channel_id=1, source_target_pairs={{0,4},{4,8},{8,12},{12,16},{16,20},{20,24},{24,28},{1,5},{5,9},{9,... | collective-permute-start | bytes 393224 | tf_op jit(solution)/shard_map/ppermute | solution.py:31
  50.4 2.5 %collective-permute-done.3 = f32[4,64,128]{2,1,0:T(8,128)S(1)} collective-permute-done((f32[4,64,128]{2,1,0:T(8,128)S(1)}, f32[4,64,128]{2,1,0:T(8,128)S(1)}, u32[]{:S(2)}, u32[]{:S(2)}) %collective-permute-start.3) | collective-permute-done | bytes 131104 | tf_op jit(solution)/shard_map/ppermute | solution.py:31
  52.9 7.4 %all_gather.6 = f32[16,64,128]{2,1,0:T(8,128)S(1)} all-gather(f32[4,64,128]{2,1,0:T(8,128)S(1)} %collective-permute-done.3), channel_id=1, replica_groups=mesh['tm'=8,'space'=4] {'space'}, dimensions={0}, use_global_device_ids=true | all-gather | bytes 655360 | tf_op jit(solution)/shard_map/all_gather | solution.py:74
  60.3 0.1 div.162
  60.4 0.4 fusion.169
  60.9 0.4 fusion.180
  61.3 0.5 fusion.190
  61.8 0.4 fusion.201
  62.2 1.5 %fusion.442 = (f32[16,64,128]{2,1,0:T(8,128)S(1)}, f32[16,64,128]{2,1,0:T(8,128)S(1)}, f32[16,64,128]{2,1,0:T(8,128)S(1)}) fusion(f32[16,64,128]{2,1,0:T(8,128)S(1)} %get-tuple-element.21, f32[16,64,128]{2,1,0:T(8,128)S(1)} %fusion.201, f32[16,64,128]{2,1,0:T(8,128)S(1)} %all_gather.6, f32[6,32,64,128]{3,2,1,0:T(8,128)} %copy-done, s32[]{:T(128)S(6)} %add.1196, ...), kind=kLoop, calls=%fused_computation.706 | loop fusion | flops 1835008 | bytes 3670024 | tf_op jit(solution)/shard_map/div | solution.py:51
  63.8 0.4 fusion.224
  64.2 0.4 fusion.235
  64.7 0.5 fusion.245
  65.1 0.4 fusion.256
  65.6 1.5 %fusion.440 = (f32[16,64,128]{2,1,0:T(8,128)S(1)}, f32[16,64,128]{2,1,0:T(8,128)S(1)}) fusion(f32[16,64,128]{2,1,0:T(8,128)S(1)} %get-tuple-element.21, f32[6,32,64,128]{3,2,1,0:T(8,128)} %copy-done, s32[]{:T(128)S(6)} %add.1193, s32[]{:T(128)S(6)} %select_n.23, f32[16,64,128]{2,1,0:T(8,128)S(1)} %fusion.256, f32[16,64,128]{2,1,0:T(8,128)S(1)} %get-tuple-element.12), kind=kLoop, calls=%fused_computation.705 | loop fusion | flops 1835008 | bytes 3145736 | tf_op jit(solution)/shard_map/div | solution.py:51
  67.1 0.4 fusion.279
  67.5 0.4 fusion.290
  68.0 0.5 fusion.300
  68.4 0.4 fusion.311
  68.9 1.5 %fusion.438 = (f32[16,64,128]{2,1,0:T(8,128)S(1)}, f32[16,64,128]{2,1,0:T(8,128)S(1)}) fusion(f32[16,64,128]{2,1,0:T(8,128)S(1)} %get-tuple-element.21, f32[6,32,64,128]{3,2,1,0:T(8,128)} %copy-done, s32[]{:T(128)S(6)} %add.1194, s32[]{:T(128)S(6)} %select_n.23, f32[16,64,128]{2,1,0:T(8,128)S(1)} %fusion.311, f32[16,64,128]{2,1,0:T(8,128)S(1)} %get-tuple-element.10), kind=kLoop, calls=%fused_computation.704 | loop fusion | flops 1835008 | bytes 3145736 | tf_op jit(solution)/shard_map/div | solution.py:51
  70.4 0.4 fusion.334
  70.8 0.4 fusion.345
  71.3 0.5 fusion.355
  71.7 0.5 fusion.436
  72.2 0.3 fusion.372
  72.6 4.4 %collective-permute-start.4 = (f32[4,64,128]{2,1,0:T(8,128)S(1)}, f32[4,64,128]{2,1,0:T(8,128)S(1)}, u32[]{:S(2)}, u32[]{:S(2)}) collective-permute-start(f32[4,64,128]{2,1,0:T(8,128)S(1)} %get-tuple-element.24), channel_id=1, source_target_pairs={{0,4},{4,8},{8,12},{12,16},{16,20},{20,24},{24,28},{1,5},{5,9},{9,... | collective-permute-start | bytes 393224 | tf_op jit(solution)/shard_map/ppermute | solution.py:31
  77.0 3.2 %collective-permute-done.4 = f32[4,64,128]{2,1,0:T(8,128)S(1)} collective-permute-done((f32[4,64,128]{2,1,0:T(8,128)S(1)}, f32[4,64,128]{2,1,0:T(8,128)S(1)}, u32[]{:S(2)}, u32[]{:S(2)}) %collective-permute-start.4) | collective-permute-done | bytes 131104 | tf_op jit(solution)/shard_map/ppermute | solution.py:31
  80.2 6.5 %all_gather.7 = f32[16,64,128]{2,1,0:T(8,128)S(1)} all-gather(f32[4,64,128]{2,1,0:T(8,128)S(1)} %collective-permute-done.4), channel_id=1, replica_groups=mesh['tm'=8,'space'=4] {'space'}, dimensions={0}, use_global_device_ids=true | all-gather | bytes 655360 | tf_op jit(solution)/shard_map/all_gather | solution.py:74
  86.7 0.1 div.186
  86.8 0.4 fusion.383
  87.2 0.4 fusion.394
  87.7 0.4 fusion.404
  88.1 0.4 fusion.415
  88.6 0.4 fusion.422
  89.0 1.3 multiply_reduce_fusion
  90.3 42.5 %psum.7 = f32[]{:T(128)} all-reduce(f32[]{:T(128)} %get-tuple-element.3), channel_id=1, replica_groups=mesh['tm'=8,'space'=4] {'tm','space'}, use_global_device_ids=true, to_apply=%region_1.2 | all-reduce | flops 1 | bytes 8 | tf_op jit(solution)/shard_map/psum | solution.py:89
  132.8 0.8 pad_maximum_fusion.1
  (14 shorter events, 0.4 us)
Async XLA Ops:
  2.7 12.2 %collective-permute-start = (f32[6,4,64,128]{3,2,1,0:T(8,128)S(1)}, f32[6,4,64,128]{3,2,1,0:T(8,128)S(1)}, u32[]{:S(2)}, u32[]{:S(2)}) collective-permute-start(f32[6,4,64,128]{3,2,1,0:T(8,128)S(1)} %pad_maximum_fusion), channel_id=1, source_target_pairs={{0,1},{1,2},{2,3},{3,0},{4,5},{5,6},{6,7},{7,4},{8,9},{9,10},{10,1... | collective-permute-start | bytes 2359304 | tf_op jit(solution)/shard_map/ppermute | solution.py:19
  14.9 11.4 %collective-permute-start.1 = (f32[6,4,64,128]{3,2,1,0:T(8,128)S(1)}, f32[6,4,64,128]{3,2,1,0:T(8,128)S(1)}, u32[]{:S(2)}, u32[]{:S(2)}) collective-permute-start(f32[6,4,64,128]{3,2,1,0:T(8,128)S(1)} %collective-permute-done), channel_id=1, source_target_pairs={{0,1},{1,2},{2,3},{3,0},{4,5},{5,6},{6,7},{7,4},{8,9},{9,10},{10,1... | collective-permute-start | bytes 2359304 | tf_op jit(solution)/shard_map/ppermute | solution.py:19
  26.3 11.4 %collective-permute-start.2 = (f32[6,4,64,128]{3,2,1,0:T(8,128)S(1)}, f32[6,4,64,128]{3,2,1,0:T(8,128)S(1)}, u32[]{:S(2)}, u32[]{:S(2)}) collective-permute-start(f32[6,4,64,128]{3,2,1,0:T(8,128)S(1)} %collective-permute-done.1), channel_id=1, source_target_pairs={{0,1},{1,2},{2,3},{3,0},{4,5},{5,6},{6,7},{7,4},{8,9},{9,10},{10,1... | collective-permute-start | bytes 2359304 | tf_op jit(solution)/shard_map/ppermute | solution.py:19
  37.8 1.0 copy-start.1
  37.8 1.1 copy-start.2
  39.2 6.9 %copy-start = (f32[6,32,64,128]{3,2,1,0:T(8,128)}, f32[6,32,64,128]{3,2,1,0:T(8,128)S(1)}, u32[]{:S(2)}) copy-start(f32[6,32,64,128]{3,2,1,0:T(8,128)S(1)} %constant_dynamic-update-slice_fusion) | copy-start | bytes 18874372
  46.2 6.7 %collective-permute-start.3 = (f32[4,64,128]{2,1,0:T(8,128)S(1)}, f32[4,64,128]{2,1,0:T(8,128)S(1)}, u32[]{:S(2)}, u32[]{:S(2)}) collective-permute-start(f32[4,64,128]{2,1,0:T(8,128)S(1)} %fusion.432), channel_id=1, source_target_pairs={{0,4},{4,8},{8,12},{12,16},{16,20},{20,24},{24,28},{1,5},{5,9},{9,... | collective-permute-start | bytes 393224 | tf_op jit(solution)/shard_map/ppermute | solution.py:31
  72.6 7.6 %collective-permute-start.4 = (f32[4,64,128]{2,1,0:T(8,128)S(1)}, f32[4,64,128]{2,1,0:T(8,128)S(1)}, u32[]{:S(2)}, u32[]{:S(2)}) collective-permute-start(f32[4,64,128]{2,1,0:T(8,128)S(1)} %get-tuple-element.24), channel_id=1, source_target_pairs={{0,4},{4,8},{8,12},{12,16},{16,20},{20,24},{24,28},{1,5},{5,9},{9,... | collective-permute-start | bytes 393224 | tf_op jit(solution)/shard_map/ppermute | solution.py:31
